TPU v7x, 32 devices: a whole 2x2x4 slice. The times are simulated.
32 devices in a mesh: dp: 4 (over y, x), tensor: 2 (over core), precond: 4 (over z).
Axes of the slice: x: 2, y: 2, z: 4, core: 2. Of those that a mesh axis runs over, the one named last changes fastest.
Arguments:
- tokens: bfloat16 [512, 8192], P('dp', 'tensor'), may hold values from -6 to 6
- gain: bfloat16 [8192], P('tensor'), may hold values from 0.099609375 to 1.8984375
- cotangent: bfloat16 [512, 12288], P('dp', 'precond'), may hold values from -6 to 6
Outputs:
- preconditioner: float32 [8, 1024, 1024], P('tensor', ('dp', 'precond'))
All inputs are finite; a program needn't handle non-finite values.
Results may differ from a plain program's by a relative error of at most 0.00089.
Values sent between devices are 32-bit elements; how exact they have to be, the bound alone decides.
No kernel may reach another device: no remote copies, remote signals or barrier semaphores. Data moves between devices by JAX's collectives and lax.ppermute only.
A program may use at most 128 MiB of HBM per device.

v0:
```python
import jax
import jax.numpy as jnp
from jax import lax
from jax.sharding import PartitionSpec as P

BLK = 1024
highest = lax.Precision.HIGHEST
epsilon = 1e-06
damping = 0.01


def batched(left_side, right_side):
    return jnp.einsum("bij,bjk->bik", left_side, right_side, precision=highest)


def body(tokens, gain, cotangent):
    values = tokens.astype(jnp.float32)
    square_part = jnp.sum(values * values, axis=1)[None, :]
    gathered = lax.all_gather(square_part, "tensor", axis=0, tiled=True)
    mean_square = jnp.sum(gathered, axis=0)[:, None] / (values.shape[1] * lax.axis_size("tensor"))
    normed = (values * lax.rsqrt(mean_square + epsilon) * gain.astype(jnp.float32)).astype(
        jnp.bfloat16
    )
    token_total = tokens.shape[0] * lax.axis_size("dp")
    partial_value = lax.dot_general(
        normed, cotangent, (((0,), (0,)), ((), ())), preferred_element_type=jnp.float32
    )
    gradient = lax.psum_scatter(partial_value, "dp", scatter_dimension=1, tiled=True) / token_total
    block_count = gradient.shape[0] // BLK
    blocks = gradient.reshape(block_count, BLK, gradient.shape[1])
    local_gram = jnp.einsum("bik,bjk->bij", blocks, blocks, precision=highest)
    identity = jnp.eye(BLK, dtype=jnp.float32)
    summed_gram = lax.psum(local_gram, ("dp", "precond"))
    statistic = summed_gram + damping * identity
    scaling = 2.0 * jnp.trace(statistic, axis1=1, axis2=2)[:, None, None] / BLK
    start_iterate = statistic / scaling
    factor_one = (5.0 * identity - start_iterate) / 4.0
    row_count = BLK // (lax.axis_size("dp") * lax.axis_size("precond"))
    offset = (
        lax.axis_index("dp") * lax.axis_size("precond") + lax.axis_index("precond")
    ) * row_count
    factor_rows = lax.dynamic_slice_in_dim(factor_one, offset, row_count, 1)
    power_two = batched(factor_rows, factor_one)
    power_three = batched(power_two, factor_one)
    power_four = batched(power_three, factor_one)
    power_five = batched(power_four, factor_one)
    product = batched(power_five, start_iterate)
    return jnp.power(scaling, -0.25) * (5.0 * factor_rows - product) / 4.0


def solution(mesh):
    in_specs = (P("dp", "tensor"), P("tensor"), P("dp", "precond"))
    out_specs = P("tensor", ("dp", "precond"), None)
    return jax.shard_map(body, mesh=mesh, in_specs=in_specs, out_specs=out_specs, check_vma=False)
```

profile of v0, /device:TPU:0, one launch (start us, length us, event | category | flops | bytes accessed | tf_op | source)
XLA Modules:
  0.0 1049.3 jit_solution(3601064974182051058)
XLA Ops:
  6.5 0.0 copy-start
  6.5 0.0 reduce-scatter.2.cloned.1.call-start
  6.5 0.8 convert_element_type.11
  7.3 1.5 fusion.2
  8.8 2.0 all-gather.1
  10.8 0.0 copy-done
  10.8 20.7 %fusion.7 = f32[4096,3072]{1,0:T(8,128)} fusion(bf16[128,3072]{1,0:T(8,128)(2,1)S(1)} %copy-done, bf16[128,4096]{1,0:T(8,128)(2,1)} %param.3, f32[4096]{0:T(1024)S(1)} %convert_element_type.11, f32[128]{0:T(128)S(1)} %add_rsqrt_fusion), kind=kOutput, calls=%fused_computation.15 | convolution fusion | flops 3223322624 | bytes 52183552 | tf_op jit(solution)/shard_map/dot_general | solution.py:25
  31.5 0.0 reduce-scatter.2.cloned.1.call-update
  31.6 0.0 all-reduce.2.cloned.1.call-start
  31.6 426.7 %reduce-scatter.2.cloned.1.call-done = f32[4096,768]{1,0:T(8,128)} async-done(((f32[4096,3072]{1,0:T(8,128)}), f32[4096,768]{1,0:T(8,128)}) %reduce-scatter.2.cloned.1.call-update) | async-done | bytes 12582928 | tf_op jit(solution)/shard_map/reduce_scatter | solution.py:28
  458.3 10.0 broadcast_multiply_fusion
  468.2 47.3 %fusion.14 = f32[4,1024,1024]{2,1,0:T(8,128)} fusion(f32[4,1024,768]{2,1,0:T(8,128)} %bitcast.13), kind=kOutput, calls=%fused_computation.24 | convolution fusion | flops 38654705664 | bytes 29360128 | tf_op jit(solution)/shard_map/bik,bjk->bij/dot_general | solution.py:31
  515.5 0.0 all-reduce.2.cloned.1.call-update
  515.6 0.3 iota_compare_fusion
  515.9 4.3 fusion
  520.2 446.5 %all-reduce.2.cloned.1.call-done = f32[4,1024,1024]{2,1,0:T(8,128)} async-done(((f32[4,1024,1024]{2,1,0:T(8,128)}), f32[4,1024,1024]{2,1,0:T(8,128)}) %all-reduce.2.cloned.1.call-update) | async-done | bytes 16777232 | tf_op jit(solution)/shard_map/psum | solution.py:33
  966.8 10.3 select_reduce_fusion
  977.0 8.1 subtract_multiply_fusion
  985.2 10.2 fusion.11
  995.4 10.4 fusion.15
  1005.8 10.4 fusion.16
  1016.2 10.3 fusion.17
  1026.5 0.0 copy-start.1
  1026.5 15.7 %fusion.6 = f32[4,64,1024]{2,1,0:T(8,128)} fusion(f32[4,64,1024]{2,1,0:T(8,128)S(1)} %fusion.17, f32[4,1024,1024]{2,1,0:T(8,128)S(1)} %subtract_multiply_fusion, s32[]{:T(128)S(6)} %select_n.9, f32[4]{0:T(128)S(1)} %get-tuple-element.5, f32[4,1024,1024]{2,1,0:T(8,128)} %all-reduce.2.cloned.1.call-done, f32[4]{0:T(128)S(1)} %get-tuple-element.6, ...), kind=kOutput, calls=%fused_computation.14 | convolution fusion | flops 3230662656 | bytes 24117284 | tf_op jit(solution)/shard_map/bij,bjk->bik/dot_general | solution.py:13
  (8 shorter events, 0.1 us)
Async XLA Ops:
  6.5 4.3 copy-start
  6.5 451.7 %reduce-scatter.2.cloned.1.call-start = ((), (), s32[]{:S(2)}) async-start(), calls=%async_computation.1 | async-start | bytes 62914560 | tf_op jit(solution)/shard_map/reduce_scatter | solution.py:28
  31.6 935.2 %all-reduce.2.cloned.1.call-start = ((), (), s32[]{:S(2)}) async-start(), calls=%async_computation.2 | async-start | bytes 33554432 | tf_op jit(solution)/shard_map/psum | solution.py:33
  966.8 10.3 copy-start.2
  966.8 10.3 copy-start.3
  1026.5 15.7 %copy-start.1 = (bf16[128,3072]{1,0:T(8,128)(2,1)S(1)}, bf16[128,3072]{1,0:T(8,128)(2,1)}, u32[]{:S(2)}) copy-start(bf16[128,3072]{1,0:T(8,128)(2,1)} %param.5) | copy-start | bytes 2359300
Sparse Core Ops, SparseCore 0:
  31.7 426.5 reduce-scatter.1
  515.7 451.0 all-reduce.1
where the time goes:
time: 1050 us
  waiting for transfers between devices  873 us (83%)
  matrix products  125 us (12%)
  other arithmetic  35.3 us (3%)
  between operations  13.8 us (1%)
    psum x1, waiting for transfers between devices, body(): summed_gram = lax.psum(local_gram, ('dp', 'precond'))  447 us
    reduce_scatter x1, waiting for transfers between devices, body(): lax.psum_scatter(partial_value, 'dp', scatter_dimension=1, tiled=True)  427 us
    dot_general x5, matrix products, batched(): return jnp.einsum('bij,bjk->bik', left_side, right_side, precision=highest)  57 us
    dot_general x1, matrix products, body(): local_gram = jnp.einsum('bik,bjk->bij', blocks, blocks, precision=highest)  47.3 us
  transfers between devices with their start and end apart: 2, of which 2 were waited for; matrix products, arithmetic and copies ran while one was open for 0% of the time, Pallas kernels for 0%

commit v1 on v0

--- a/solution.py
+++ b/solution.py
@@ -30,7 +30,7 @@
     blocks = gradient.reshape(block_count, BLK, gradient.shape[1])
     local_gram = jnp.einsum("bik,bjk->bij", blocks, blocks, precision=highest)
     identity = jnp.eye(BLK, dtype=jnp.float32)
-    summed_gram = lax.psum(local_gram, ("dp", "precond"))
+    summed_gram = lax.psum(lax.psum(local_gram, "precond"), "dp")
     statistic = summed_gram + damping * identity
     scaling = 2.0 * jnp.trace(statistic, axis1=1, axis2=2)[:, None, None] / BLK
     start_iterate = statistic / scaling

time: 1050 us -> 1470 us (1.40)
  waiting for transfers between devices: 873 us -> 1290 us
    psum x1 -> x2, waiting for transfers between devices: 447 us -> 867 us  [body(): summed_gram = lax.psum(lax.psum(local_gram, 'precond'), 'dp')]
  transfers between devices with their start and end apart: 2 -> 3, of which waited for: 2 -> 3; matrix products, arithmetic and copies ran while one was open for 0% -> 0% of each run, Pallas kernels for 0% -> 0%
where the time goes in v1:
time: 1470 us
  waiting for transfers between devices  1290 us (88%)
  matrix products  125 us (9%)
  other arithmetic  35.3 us (2%)
    psum x2, waiting for transfers between devices, body(): summed_gram = lax.psum(lax.psum(local_gram, 'precond'), 'dp')  867 us
    reduce_scatter x1, waiting for transfers between devices, body(): lax.psum_scatter(partial_value, 'dp', scatter_dimension=1, tiled=True)  426 us
    dot_general x5, matrix products, batched(): return jnp.einsum('bij,bjk->bik', left_side, right_side, precision=highest)  57 us
    dot_general x1, matrix products, body(): local_gram = jnp.einsum('bik,bjk->bij', blocks, blocks, precision=highest)  47.2 us
  transfers between devices with their start and end apart: 3, of which 3 were waited for; matrix products, arithmetic and copies ran while one was open for 0% of the time, Pallas kernels for 0%

profile of v1, /device:TPU:0, one launch (start us, length us, event | category | flops | bytes accessed | tf_op | source)
XLA Modules:
  0.0 1469.8 jit_solution(11345556893335817440)
XLA Ops:
  6.5 0.8 convert_element_type.11
  7.3 1.5 fusion.2
  8.8 2.0 all-gather.1
  10.8 20.7 %fusion.7 = f32[4096,3072]{1,0:T(8,128)} fusion(bf16[128,3072]{1,0:T(8,128)(2,1)S(1)} %copy-done, bf16[128,4096]{1,0:T(8,128)(2,1)} %param.3, f32[4096]{0:T(1024)S(1)} %convert_element_type.11, f32[128]{0:T(128)S(1)} %add_rsqrt_fusion), kind=kOutput, calls=%fused_computation.15 | convolution fusion | flops 3223322624 | bytes 52183552 | tf_op jit(solution)/shard_map/dot_general | solution.py:25
  31.5 0.0 reduce-scatter.2.cloned.1.call-update
  31.6 0.2 all-reduce.3.cloned.1.call-start
  31.8 426.5 %reduce-scatter.2.cloned.1.call-done = f32[4096,768]{1,0:T(8,128)} async-done(((f32[4096,3072]{1,0:T(8,128)}), f32[4096,768]{1,0:T(8,128)}) %reduce-scatter.2.cloned.1.call-update) | async-done | bytes 12582928 | tf_op jit(solution)/shard_map/reduce_scatter | solution.py:28
  458.3 10.0 broadcast_multiply_fusion
  468.2 47.2 %fusion.14 = f32[4,1024,1024]{2,1,0:T(8,128)} fusion(f32[4,1024,768]{2,1,0:T(8,128)} %bitcast.13), kind=kOutput, calls=%fused_computation.24 | convolution fusion | flops 38654705664 | bytes 29360128 | tf_op jit(solution)/shard_map/bik,bjk->bij/dot_general | solution.py:31
  515.4 0.0 all-reduce.3.cloned.1.call-update
  515.4 0.0 all-reduce.5.cloned.1.call-start
  515.5 562.3 %all-reduce.3.cloned.1.call-done = f32[4,1024,1024]{2,1,0:T(8,128)} async-done(((f32[4,1024,1024]{2,1,0:T(8,128)}), f32[4,1024,1024]{2,1,0:T(8,128)}) %all-reduce.3.cloned.1.call-update) | async-done | bytes 16777232 | tf_op jit(solution)/shard_map/psum | solution.py:33
  1077.7 0.0 all-reduce.5.cloned.1.call-update
  1077.7 0.3 iota_compare_fusion
  1078.1 4.3 fusion
  1082.4 305.2 %all-reduce.5.cloned.1.call-done = f32[4,1024,1024]{2,1,0:T(8,128)} async-done(((f32[4,1024,1024]{2,1,0:T(8,128)}), f32[4,1024,1024]{2,1,0:T(8,128)}) %all-reduce.5.cloned.1.call-update) | async-done | bytes 16777232 | tf_op jit(solution)/shard_map/psum | solution.py:33
  1387.6 10.3 select_reduce_fusion
  1397.9 8.1 subtract_multiply_fusion
  1406.0 10.2 fusion.11
  1416.2 10.4 fusion.15
  1426.6 10.4 fusion.16
  1437.1 10.3 fusion.17
  1447.3 0.0 copy-start.1
  1447.3 15.7 %fusion.6 = f32[4,64,1024]{2,1,0:T(8,128)} fusion(f32[4,64,1024]{2,1,0:T(8,128)S(1)} %fusion.17, f32[4,1024,1024]{2,1,0:T(8,128)S(1)} %subtract_multiply_fusion, s32[]{:T(128)S(6)} %select_n.9, f32[4]{0:T(128)S(1)} %get-tuple-element.5, f32[4,1024,1024]{2,1,0:T(8,128)} %all-reduce.5.cloned.1.call-done, f32[4]{0:T(128)S(1)} %get-tuple-element.6, ...), kind=kOutput, calls=%fused_computation.14 | convolution fusion | flops 3230662656 | bytes 24117284 | tf_op jit(solution)/shard_map/bij,bjk->bik/dot_general | solution.py:13
  (11 shorter events, 0.1 us)
Async XLA Ops:
  6.5 4.3 copy-start
  6.5 451.7 %reduce-scatter.2.cloned.1.call-start = ((), (), s32[]{:S(2)}) async-start(), calls=%async_computation.1 | async-start | bytes 62914560 | tf_op jit(solution)/shard_map/reduce_scatter | solution.py:28
  31.6 1046.2 %all-reduce.3.cloned.1.call-start = ((), (), s32[]{:S(2)}) async-start(), calls=%async_computation.2 | async-start | bytes 33554432 | tf_op jit(solution)/shard_map/psum | solution.py:33
  515.4 872.2 %all-reduce.5.cloned.1.call-start = ((), (), s32[]{:S(2)}) async-start(), calls=%async_computation.3 | async-start | bytes 33554432 | tf_op jit(solution)/shard_map/psum | solution.py:33
  1387.6 10.3 copy-start.2
  1387.6 10.3 copy-start.3
  1447.3 15.7 %copy-start.1 = (bf16[128,3072]{1,0:T(8,128)(2,1)S(1)}, bf16[128,3072]{1,0:T(8,128)(2,1)}, u32[]{:S(2)}) copy-start(bf16[128,3072]{1,0:T(8,128)(2,1)} %param.5) | copy-start | bytes 2359300
Sparse Core Ops, SparseCore 0:
  31.7 426.5 reduce-scatter.1
  515.5 562.1 all-reduce.2
  1081.3 306.2 all-reduce.4
